TPU v7x, 32 devices: a whole 2x2x4 slice. The times are simulated.
32 devices in a mesh: field: 2 (over x), expo: 8 (over z, y), sky: 2 (over core).
Axes of the slice: x: 2, y: 2, z: 4, core: 2. Of those that a mesh axis runs over, the one named last changes fastest.
Arguments:
- science: float32 [64, 64, 512], P(('field', 'expo'), 'sky'), parts along dimension 0, may hold values from -6 to 6
- inv_variance: float32 [64, 64, 512], P(('field', 'expo'), 'sky'), parts along dimension 0, may hold values from 0.25 to 4
- pixel_masks: int32 [64, 64, 512], P(('field', 'expo'), 'sky'), parts along dimension 0, may hold values 0 or 1
- point_spread: float32 [64, 5, 5], P(('field', 'expo')), parts along dimension 0, may hold values from 0.02 to 0.1
- tile_offset: int32 [8, 32], P(None, 'expo'), may hold values from 0 to 1
- column_shift: int32 [8, 32], P(None, 'expo'), may hold values from -128 to 128
- trail_kernel: float32 [8, 3, 3], P('expo'), may hold values from 0.1 to 1
Outputs:
- likelihood: float32 [16, 64, 512], P(('field', 'expo'), 'sky'), parts along dimension 0
There are 2 independent parts, one for each index of `field`. A program takes and returns all parts, laid end to end along the dimension named above; an argument that names none is the same for every part. Nothing has to cross between parts.
All inputs are finite; a program needn't handle non-finite values. No bound on the sum of `pixel_masks` on one device may be relied on, other than what follows from the above.
Results may differ from a plain program's by a relative error of at most 0.0003.
Values sent between devices are 32-bit elements; how exact they have to be, the bound alone decides.
No kernel may reach another device: no remote copies, remote signals or barrier semaphores. Data moves between devices by JAX's collectives and lax.ppermute only.
A program may use at most 128 MiB of HBM per device.

v0:
```python
import functools

import jax
import jax.numpy as jnp
from jax import lax
from jax.experimental import pallas as pl
from jax.experimental.pallas import tpu as pltpu
from jax.sharding import PartitionSpec as P


MAX_SHIFT = 128
LANES = 128
SUB = 8


def lane_shifted(pieces, lane, offset):
    if offset == 0:
        return pieces
    count = len(pieces)
    rolled = [pltpu.roll(piece, (-offset) % LANES, 1) for piece in pieces]
    out = []
    for c in range(count):
        near = rolled[c]
        if offset > 0:
            far = rolled[c + 1] if c + 1 < count else jnp.zeros_like(near)
            out.append(jnp.where(lane < LANES - offset, near, far))
        else:
            far = rolled[c - 1] if c > 0 else jnp.zeros_like(near)
            out.append(jnp.where(lane >= -offset, near, far))
    return out


def filter_rows(load, taps, row_taps, chunks, lane):
    half = row_taps // 2
    columns = [[None] * chunks for _ in range(row_taps)]
    for c in range(chunks):
        rows = [load(a, c) for a in range(row_taps)]
        for b in range(row_taps):
            total = rows[0] * taps[0][b]
            for a in range(1, row_taps):
                total = total + rows[a] * taps[a][b]
            columns[b][c] = total
    result = columns[half]
    for b in range(row_taps):
        if b != half:
            moved = lane_shifted(columns[b], lane, b - half)
            result = [x + y for x, y in zip(result, moved)]
    return result


def filter_groups(image, wide, taps_of, first, count, exposures, chunks, taps, lane):
    half = taps // 2
    for e in range(exposures):
        for k in range(2):
            scale = taps_of(e, k)
            for g in range(count):
                row = pl.multiple_of((first + g) * SUB, SUB)

                def load(a, c):
                    return image[k, e, c, pl.ds(row + (SUB + a - half), SUB), :]

                result = filter_rows(load, scale, taps, chunks, lane)
                for c in range(chunks):
                    wide[e, k, 1 + c, pl.ds(row, SUB), :] = result[c]


def taps_in(spread_ref, taps):
    def taps_of(e, k):
        scale = [[spread_ref[a, e, b] for b in range(taps)] for a in range(taps)]
        return scale if k == 0 else [[x * x for x in line] for line in scale]

    return taps_of


def near_kernel(spread_ref, own_ref, image, wide, *, rows, chunks, taps):
    exposures = own_ref.shape[1]
    sky = lax.axis_index("sky")
    lane = lax.broadcasted_iota(jnp.int32, (SUB, LANES), 1)
    zero = jnp.zeros((SUB, LANES), jnp.float32)
    base = pl.multiple_of(SUB + rows * sky, SUB)
    for k in range(2):
        for e in range(exposures):
            for c in range(chunks):
                image[k, e, c, 0:SUB, :] = zero
                image[k, e, c, SUB + 2 * rows :, :] = zero
                image[k, e, c, pl.ds(base, rows), :] = own_ref[k, e, :, c * LANES : (c + 1) * LANES]
    inside = rows // SUB - 1
    first = (2 * (rows // SUB) - inside) * sky
    filter_groups(image, wide, taps_in(spread_ref, taps), first, inside, exposures, chunks, taps, lane)
    blank = jnp.zeros((2 * rows, LANES), jnp.float32)
    for e in range(exposures):
        for k in range(2):
            for c in (0, chunks + 1, chunks + 2):
                wide[e, k, c] = blank


def stack_velocity(out, p, v, wide, edge, offset_ref, shift_ref, sky, rows, chunks, lane):
    exposures = wide.shape[0]
    totals = [None, None]
    edges = None
    groups = rows // SUB
    for e in range(exposures):
        tile = lax.rem(sky + offset_ref[e, v], 2)
        start = MAX_SHIFT - shift_ref[e, v]
        skip = lax.div(start, LANES)
        turn = lax.rem(start, LANES)
        back = lax.rem(LANES - turn, LANES)
        keep = lane < LANES - turn
        base = pl.multiple_of(tile * rows, SUB)
        for k in range(2):
            moved = [
                [
                    pltpu.roll(wide[e, k, skip + c, pl.ds(pl.multiple_of(base + g * SUB, SUB), SUB), :], back, 1)
                    for g in range(groups)
                ]
                for c in range(chunks + 1)
            ]
            picked = [
                [jnp.where(keep, moved[c][g], moved[c + 1][g]) for g in range(groups)] for c in range(chunks)
            ]
            if totals[k] is None:
                totals[k] = picked
            else:
                totals[k] = [[x + y for x, y in zip(p0, p1)] for p0, p1 in zip(totals[k], picked)]
        moved = [pltpu.roll(edge[e, 1 - tile, skip + c], back, 1) for c in range(chunks + 1)]
        picked = [jnp.where(keep, moved[c], moved[c + 1]) for c in range(chunks)]
        edges = picked if edges is None else [x + y for x, y in zip(edges, picked)]
    for k in range(2):
        for c in range(chunks):
            for g in range(groups):
                row = (k * chunks + c) * rows + g * SUB
                out[p, row : row + SUB, :] = totals[k][c][g]
    for c in range(chunks):
        row = 2 * chunks * rows + 2 * c
        out[p, row : row + 2, :] = edges[c][0:2, :]


def stack_targets(outs, hops, inner, wide, edge, offset_ref, shift_ref, sky, rows, chunks, lane):
    me = lax.axis_index("expo")
    count = lax.axis_size("expo")
    for out, hop in zip(outs, hops):
        owner = target_of(me, hop, count, inner)
        for p in range(out.shape[0]):
            stack_velocity(
                out, p, owner * out.shape[0] + p, wide, edge, offset_ref, shift_ref, sky, rows, chunks, lane
            )


def target_of(index, hop, count, inner):
    far, near = hop
    outer = count // inner
    low = lax.rem(index, inner)
    high = lax.div(index, inner)
    if outer & (outer - 1) == 0:
        high = lax.bitwise_xor(high, jnp.int32(far))
    else:
        high = lax.rem(high + far, outer)
    return high * inner + lax.rem(low + near, inner)


def owner_index(index, hop, count, inner):
    far, near = hop
    outer = count // inner
    high, low = divmod(index, inner)
    high = high ^ far if outer & (outer - 1) == 0 else (high + far) % outer
    return high * inner + (low + near) % inner


def far_kernel(
    spread_ref, offset_ref, shift_ref, other_ref, image_in, wide_in, image, wide, edge, *outs,
    hops, inner, rows, chunks, taps,
):
    exposures = other_ref.shape[1]
    sky = lax.axis_index("sky")
    lane = lax.broadcasted_iota(jnp.int32, (SUB, LANES), 1)
    zero = jnp.zeros((SUB, LANES), jnp.float32)
    base = pl.multiple_of(SUB + rows * (1 - sky), SUB)
    for k in range(2):
        for e in range(exposures):
            for c in range(chunks):
                image[k, e, c, pl.ds(base, rows), :] = other_ref[k, e, :, c * LANES : (c + 1) * LANES]
    inside = rows // SUB - 1
    filter_groups(
        image, wide, taps_in(spread_ref, taps), inside * (1 - sky), 2 * (rows // SUB) - inside,
        exposures, chunks, taps, lane,
    )
    at_row = (rows - 1) * sky
    for e in range(exposures):
        for t in range(2):
            for c in (0, chunks + 1, chunks + 2):
                edge[e, t, c] = zero
            for k in range(2):
                for c in range(chunks):
                    edge[e, t, 1 + c, k : k + 1, :] = wide[e, k, 1 + c, pl.ds(rows * t + at_row, 1), :]
    stack_targets(outs, hops, inner, wide, edge, offset_ref, shift_ref, sky, rows, chunks, lane)


def rest_kernel(offset_ref, shift_ref, wide, edge, *outs, hops, inner, rows, chunks):
    sky = lax.axis_index("sky")
    lane = lax.broadcasted_iota(jnp.int32, (SUB, LANES), 1)
    stack_targets(outs, hops, inner, wide, edge, offset_ref, shift_ref, sky, rows, chunks, lane)


def trail_kernel_body(trail_ref, *rest, rows, chunks, taps):
    parts = rest[:-2]
    out, image = rest[-2:]
    sky = lax.axis_index("sky")
    lane = lax.broadcasted_iota(jnp.int32, (SUB, LANES), 1)
    zero = jnp.zeros((SUB, LANES), jnp.float32)
    half = taps // 2
    groups = rows // SUB
    for p in range(out.shape[0]):
        def total(row, count):
            value = parts[0][p, row : row + count, :]
            for part in parts[1:]:
                value = value + part[p, row : row + count, :]
            return value

        results = []
        edges = total(2 * chunks * rows, 2 * chunks)
        for k in range(2):
            for c in range(chunks):
                image[c, 0:SUB, :] = zero
                image[c, SUB + rows :, :] = zero
                for g in range(groups):
                    image[c, SUB + g * SUB : SUB + (g + 1) * SUB, :] = total((k * chunks + c) * rows + g * SUB, SUB)
                at = jnp.where(sky == 0, SUB + rows, SUB - 1)
                image[c, pl.ds(at, 1), :] = edges[2 * c + k : 2 * c + k + 1, :]
            scale = [[trail_ref[a, p, b] for b in range(taps)] for a in range(taps)]
            if k == 1:
                scale = [[x * x for x in line] for line in scale]
            kind = []
            for g in range(groups):
                def load(a, c):
                    return image[c, SUB + g * SUB + a - half : SUB + g * SUB + a - half + SUB, :]

                kind.append(filter_rows(load, scale, taps, chunks, lane))
            results.append(kind)
        for g in range(groups):
            for c in range(chunks):
                value = results[0][g][c] / jnp.sqrt(results[1][g][c] + 1.0)
                out[p, g * SUB : (g + 1) * SUB, c * LANES : (c + 1) * LANES] = value


SMEM = pl.BlockSpec(memory_space=pltpu.SMEM)
VMEM = pl.BlockSpec(memory_space=pltpu.VMEM)


def call(body, outputs, inputs, scratch=(), aliases={}, megabytes=8):
    return pl.pallas_call(
        body,
        out_shape=[jax.ShapeDtypeStruct(shape, jnp.float32) for shape in outputs],
        in_specs=[spec for spec, _ in inputs],
        out_specs=[VMEM] * len(outputs),
        scratch_shapes=scratch,
        input_output_aliases=aliases,
        compiler_params=pltpu.CompilerParams(vmem_limit_bytes=megabytes * 1024 * 1024),
    )(*[value for _, value in inputs])


def steps(
    science, inv_variance, pixel_masks, point_spread, tile_offset, column_shift, trail_kernel
):
    exposures, rows, width = science.shape
    chunks = width // LANES
    taps = point_spread.shape[-1]
    trail_taps = trail_kernel.shape[-1]
    count = lax.axis_size("expo")
    per = tile_offset.shape[0] // count
    inner = 2 if count % 2 == 0 else 1
    outer = count // inner

    weighted = inv_variance * pixel_masks.astype(jnp.float32)
    own = jnp.stack([science * weighted, weighted])
    other = lax.ppermute(own, "sky", [(0, 1), (1, 0)])

    spread = (SMEM, jnp.transpose(point_spread, (1, 0, 2)))
    offsets = (SMEM, tile_offset.T)
    shifts = (SMEM, column_shift.T)
    image_shape = (2, exposures, chunks, 2 * rows + 2 * SUB, LANES)
    wide_shape = (exposures, 2, chunks + 3, 2 * rows, LANES)
    edge_shape = (exposures, 2, chunks + 3, SUB, LANES)
    part = (per, 2 * chunks * rows + 2 * chunks, LANES)

    image, wide = call(
        functools.partial(near_kernel, rows=rows, chunks=chunks, taps=taps),
        [image_shape, wide_shape], [spread, (VMEM, own)],
    )
    far_order = far_first(outer)
    sends = [(d, i) for d in far_order for i in range(1, inner)]
    keeps = [(d, 0) for d in far_order]
    early = sends[:2] if inner > 1 else keeps[:1]
    late = [hop for hop in keeps + sends if hop not in early]
    late = sorted(late, key=lambda hop: far_order.index(hop[0]))
    results = call(
        functools.partial(far_kernel, hops=early, inner=inner, rows=rows, chunks=chunks, taps=taps),
        [image_shape, wide_shape, edge_shape] + [part] * len(early),
        [spread, offsets, shifts, (VMEM, other), (VMEM, image), (VMEM, wide)],
        aliases={4: 0, 5: 1},
    )
    wide, edge = results[1:3]
    parts = dict(zip(early, results[3:]))
    results = call(
        functools.partial(rest_kernel, hops=late, inner=inner, rows=rows, chunks=chunks),
        [part] * len(late), [offsets, shifts, (VMEM, wide), (VMEM, edge)],
    )
    parts.update(zip(late, results))

    def hop_pairs(hop):
        return [(i, int(owner_index(i, hop, count, inner))) for i in range(count)]

    arrived = []
    for d in far_order:
        total = parts[(d, 0)]
        for i in range(1, inner):
            moved = lax.ppermute(parts[(d, i)], "expo", hop_pairs((0, i)))
            total = total + moved
        if d:
            total = lax.ppermute(total, "expo", hop_pairs((d, 0)))
        arrived.append(total)

    return call(
        functools.partial(trail_kernel_body, rows=rows, chunks=chunks, taps=trail_taps),
        [(per, rows, width)],
        [(SMEM, jnp.transpose(trail_kernel, (1, 0, 2)))] + [(VMEM, value) for value in arrived],
        scratch=[pltpu.VMEM((chunks, rows + 2 * SUB, LANES), jnp.float32)],
    )[0]


def far_first(outer):
    return sorted(range(outer), key=lambda d: (2 * d < outer, d if 2 * d >= outer else -d))


def solution(mesh):
    return jax.shard_map(
        steps,
        mesh=mesh,
        in_specs=(
            P(("field", "expo"), "sky", None),
            P(("field", "expo"), "sky", None),
            P(("field", "expo"), "sky", None),
            P(("field", "expo"), None, None),
            P(None, "expo"),
            P(None, "expo"),
            P("expo", None, None),
        ),
        out_specs=P(("field", "expo"), "sky", None),
        check_vma=False,
    )
```

profile of v0, /device:TPU:0, one launch (start us, length us, event | category | flops | bytes accessed | tf_op | source)
XLA Modules:
  0.0 31.8 jit_solution(2728154204826424172)
XLA Ops:
  0.0 0.0 copy-start
  0.0 0.0 copy-start.2
  0.0 0.0 copy-start.1
  0.0 1.2 %multiply_bitcast_fusion = (f32[1,4,32,512]{3,2,1,0:T(8,128)S(1)}, f32[1,4,32,512]{3,2,1,0:T(8,128)S(1)}) fusion(f32[4,32,512]{2,1,0:T(8,128)} %param.7, f32[4,32,512]{2,1,0:T(8,128)} %param.8, s32[4,32,512]{2,1,0:T(8,128)} %param.9), kind=kLoop, calls=%fused_computation.1 | loop fusion | flops 196608 | bytes 1310720 | tf_op jit(solution)/shard_map/stack | solution.py:274
  1.3 0.6 %collective-permute-start = (f32[2,4,32,512]{3,2,1,0:T(8,128)S(1)}, f32[2,4,32,512]{3,2,1,0:T(8,128)S(1)}, u32[]{:S(2)}, u32[]{:S(2)}) collective-permute-start(f32[2,4,32,512]{3,2,1,0:T(8,128)S(1)} %pad_maximum_fusion.own_ref), channel_id=1, source_target_pairs={{0,1},{1,0},{2,3},{3,2},{4,5},{5,4},{6,7},{7,6},{8,9},{9,8},{10,11... | collective-permute-start | bytes 1572872 | tf_op jit(solution)/shard_map/ppermute | solution.py:275
  1.8 0.0 copy-done
  1.8 1.5 %shard_map.73 = (f32[2,4,4,80,128]{4,3,2,1,0:T(8,128)S(1)}, f32[4,2,7,64,128]{4,3,2,1,0:T(8,128)S(1)}) custom-call(f32[5,4,5]{2,1,0:T(4,128)S(1)} %bitcast.8, f32[2,4,32,512]{3,2,1,0:T(8,128)S(1)} %pad_maximum_fusion.own_ref), custom_call_target="tpu_custom_call" | custom-call | tf_op jit(solution)/shard_map/pallas_call | solution.py:250
  3.4 0.0 collective-permute-done.other_ref
  3.4 0.0 copy-done.2
  3.4 0.0 copy-done.1
  3.4 2.5 %shard_map.74 = (f32[2,4,4,80,128]{4,3,2,1,0:T(8,128)S(1)}, f32[4,2,7,64,128]{4,3,2,1,0:T(8,128)S(1)}, f32[4,2,7,8,128]{4,3,2,1,0:T(8,128)S(1)}, f32[1,264,128]{2,1,0:T(8,128)S(1)}, f32[1,264,128]{2,1,0:T(8,128)S(1)}) custom-call(f32[5,4,5]{2,1,0:T(4,128)S(1)} %bitcast.9, s32[4,8]{1,0:T(4,128)S(1)} %bitcast.10, ...), custom_call_target="tpu_custom_call", output_to_operand_aliasing={{0}: (4, {}), {1}: (5, {})} | custom-call | tf_op jit(solution)/shard_map/pallas_call | solution.py:250
  5.9 0.0 copy-start.3
  5.9 1.8 %shard_map.75 = (f32[1,264,128]{2,1,0:T(8,128)S(1)}, f32[1,264,128]{2,1,0:T(8,128)S(1)}, f32[1,264,128]{2,1,0:T(8,128)S(1)}, f32[1,264,128]{2,1,0:T(8,128)S(1)},...) custom-call(s32[4,8]{1,0:T(4,128)S(1)} %bitcast.11, s32[4,8]{1,0:T(4,128)S(1)} %bitcast.13, ...), custom_call_target="tpu_custom_call" | custom-call | tf_op jit(solution)/shard_map/pallas_call | solution.py:250
  7.8 2.9 %collective-permute-start.5 = (f32[1,264,128]{2,1,0:T(8,128)S(1)}, f32[1,264,128]{2,1,0:T(8,128)S(1)}, u32[]{:S(2)}, u32[]{:S(2)}) collective-permute-start(f32[1,264,128]{2,1,0:T(8,128)S(1)} %get-tuple-element.26), channel_id=1, source_target_pairs={{0,2},{2,0},{4,6},{6,4},{8,10},{10,8},{12,14},{14,12},{1,3},{3,1},... | collective-permute-start | bytes 405512 | tf_op jit(solution)/shard_map/ppermute | solution.py:316
  10.7 0.1 collective-permute-start.1
  10.7 1.9 %collective-permute-start.3 = (f32[1,264,128]{2,1,0:T(8,128)S(1)}, f32[1,264,128]{2,1,0:T(8,128)S(1)}, u32[]{:S(2)}, u32[]{:S(2)}) collective-permute-start(f32[1,264,128]{2,1,0:T(8,128)S(1)} %get-tuple-element.24), channel_id=1, source_target_pairs={{0,2},{2,0},{4,6},{6,4},{8,10},{10,8},{12,14},{14,12},{1,3},{3,1},... | collective-permute-start | bytes 405512 | tf_op jit(solution)/shard_map/ppermute | solution.py:316
  12.7 0.1 collective-permute-start.7
  12.8 2.3 %collective-permute-done.5 = f32[1,264,128]{2,1,0:T(8,128)S(1)} collective-permute-done((f32[1,264,128]{2,1,0:T(8,128)S(1)}, f32[1,264,128]{2,1,0:T(8,128)S(1)}, u32[]{:S(2)}, u32[]{:S(2)}) %collective-permute-start.5) | collective-permute-done | bytes 135200 | tf_op jit(solution)/shard_map/ppermute | solution.py:316
  15.1 2.1 %collective-permute-start.6 = (f32[1,264,128]{2,1,0:T(8,128)S(1)}, f32[1,264,128]{2,1,0:T(8,128)S(1)}, u32[]{:S(2)}, u32[]{:S(2)}) collective-permute-start(f32[1,264,128]{2,1,0:T(8,128)S(1)} %add.14), channel_id=1, source_target_pairs={{0,4},{2,6},{4,0},{6,2},{8,12},{10,14},{12,8},{14,10},{1,5},{3,7},... | collective-permute-start | bytes 405512 | tf_op jit(solution)/shard_map/ppermute | solution.py:319
  17.3 0.7 %collective-permute-done.1 = f32[1,264,128]{2,1,0:T(8,128)S(1)} collective-permute-done((f32[1,264,128]{2,1,0:T(8,128)S(1)}, f32[1,264,128]{2,1,0:T(8,128)S(1)}, u32[]{:S(2)}, u32[]{:S(2)}) %collective-permute-start.1) | collective-permute-done | bytes 135200 | tf_op jit(solution)/shard_map/ppermute | solution.py:316
  18.0 3.2 %collective-permute-start.2 = (f32[1,264,128]{2,1,0:T(8,128)S(1)}, f32[1,264,128]{2,1,0:T(8,128)S(1)}, u32[]{:S(2)}, u32[]{:S(2)}) collective-permute-start(f32[1,264,128]{2,1,0:T(8,128)S(1)} %add.12), channel_id=1, source_target_pairs={{0,8},{2,10},{4,12},{6,14},{8,0},{10,2},{12,4},{14,6},{1,9},{3,11}... | collective-permute-start | bytes 405512 | tf_op jit(solution)/shard_map/ppermute | solution.py:319
  21.2 0.0 collective-permute-done.3
  21.2 3.9 %collective-permute-start.4 = (f32[1,264,128]{2,1,0:T(8,128)S(1)}, f32[1,264,128]{2,1,0:T(8,128)S(1)}, u32[]{:S(2)}, u32[]{:S(2)}) collective-permute-start(f32[1,264,128]{2,1,0:T(8,128)S(1)} %add.13), channel_id=1, source_target_pairs={{0,12},{2,14},{4,8},{6,10},{8,4},{10,6},{12,0},{14,2},{1,13},{3,15... | collective-permute-start | bytes 405512 | tf_op jit(solution)/shard_map/ppermute | solution.py:319
  25.1 0.0 collective-permute-done.7
  25.1 0.0 collective-permute-done.6.rest_2_
  25.1 5.3 %collective-permute-done.2.rest_0_ = f32[1,264,128]{2,1,0:T(8,128)S(1)} collective-permute-done((f32[1,264,128]{2,1,0:T(8,128)S(1)}, f32[1,264,128]{2,1,0:T(8,128)S(1)}, u32[]{:S(2)}, u32[]{:S(2)}) %collective-permute-start.2) | collective-permute-done | bytes 135200 | tf_op jit(solution)/shard_map/ppermute | solution.py:319
  30.4 0.0 collective-permute-done.4.rest_1_
  30.4 0.0 copy-done.3
  30.4 1.4 %shard_map.76 = f32[1,32,512]{2,1,0:T(8,128)} custom-call(f32[3,1,3]{2,1,0:T(1,128)S(1)} %bitcast.14, f32[1,264,128]{2,1,0:T(8,128)S(1)} %collective-permute-done.2.rest_0_, f32[1,264,128]{2,1,0:T(8,128)S(1)} %collective-permute-done.4.rest_1_, f32[1,264,128]{2,1,0:T(8,128)S(1)} %collective-permute-done.6.rest_2_, f32[1,264,128]{2,1,0:T(8,128)S(1)} %add.15.rest_3_), custom_call_target="tpu_custom_call" | custom-call | tf_op jit(solution)/shard_map/pallas_call | solution.py:250
  (5 shorter events, 0.1 us)
Async XLA Ops:
  0.0 1.8 %copy-start = (f32[4,5,5]{2,0,1:T(4,128)S(1)}, f32[4,5,5]{2,0,1:T(4,128)}, u32[]{:S(2)}) copy-start(f32[4,5,5]{2,0,1:T(4,128)} %param.10) | copy-start | bytes 1204
  0.0 3.4 %copy-start.2 = (s32[8,4]{0,1:T(4,128)S(1)}, s32[8,4]{0,1:T(4,128)}, u32[]{:S(2)}) copy-start(s32[8,4]{0,1:T(4,128)} %param.12) | copy-start | bytes 388
  0.0 3.4 %copy-start.1 = (s32[8,4]{0,1:T(4,128)S(1)}, s32[8,4]{0,1:T(4,128)}, u32[]{:S(2)}) copy-start(s32[8,4]{0,1:T(4,128)} %param.11) | copy-start | bytes 388
  1.3 2.1 %collective-permute-start = (f32[2,4,32,512]{3,2,1,0:T(8,128)S(1)}, f32[2,4,32,512]{3,2,1,0:T(8,128)S(1)}, u32[]{:S(2)}, u32[]{:S(2)}) collective-permute-start(f32[2,4,32,512]{3,2,1,0:T(8,128)S(1)} %pad_maximum_fusion.own_ref), channel_id=1, source_target_pairs={{0,1},{1,0},{2,3},{3,2},{4,5},{5,4},{6,7},{7,6},{8,9},{9,8},{10,11... | collective-permute-start | bytes 1572872 | tf_op jit(solution)/shard_map/ppermute | solution.py:275
  5.9 24.5 %copy-start.3 = (f32[1,3,3]{2,0,1:T(1,128)S(1)}, f32[1,3,3]{2,0,1:T(1,128)}, u32[]{:S(2)}) copy-start(f32[1,3,3]{2,0,1:T(1,128)} %param.13) | copy-start | bytes 112
  7.8 7.3 %collective-permute-start.5 = (f32[1,264,128]{2,1,0:T(8,128)S(1)}, f32[1,264,128]{2,1,0:T(8,128)S(1)}, u32[]{:S(2)}, u32[]{:S(2)}) collective-permute-start(f32[1,264,128]{2,1,0:T(8,128)S(1)} %get-tuple-element.26), channel_id=1, source_target_pairs={{0,2},{2,0},{4,6},{6,4},{8,10},{10,8},{12,14},{14,12},{1,3},{3,1},... | collective-permute-start | bytes 405512 | tf_op jit(solution)/shard_map/ppermute | solution.py:316
  10.7 7.3 %collective-permute-start.1 = (f32[1,264,128]{2,1,0:T(8,128)S(1)}, f32[1,264,128]{2,1,0:T(8,128)S(1)}, u32[]{:S(2)}, u32[]{:S(2)}) collective-permute-start(f32[1,264,128]{2,1,0:T(8,128)S(1)} %get-tuple-element.22), channel_id=1, source_target_pairs={{0,2},{2,0},{4,6},{6,4},{8,10},{10,8},{12,14},{14,12},{1,3},{3,1},... | collective-permute-start | bytes 405512 | tf_op jit(solution)/shard_map/ppermute | solution.py:316
  10.7 10.4 %collective-permute-start.3 = (f32[1,264,128]{2,1,0:T(8,128)S(1)}, f32[1,264,128]{2,1,0:T(8,128)S(1)}, u32[]{:S(2)}, u32[]{:S(2)}) collective-permute-start(f32[1,264,128]{2,1,0:T(8,128)S(1)} %get-tuple-element.24), channel_id=1, source_target_pairs={{0,2},{2,0},{4,6},{6,4},{8,10},{10,8},{12,14},{14,12},{1,3},{3,1},... | collective-permute-start | bytes 405512 | tf_op jit(solution)/shard_map/ppermute | solution.py:316
  12.7 12.4 %collective-permute-start.7 = (f32[1,264,128]{2,1,0:T(8,128)S(1)}, f32[1,264,128]{2,1,0:T(8,128)S(1)}, u32[]{:S(2)}, u32[]{:S(2)}) collective-permute-start(f32[1,264,128]{2,1,0:T(8,128)S(1)} %get-tuple-element.28), channel_id=1, source_target_pairs={{0,2},{2,0},{4,6},{6,4},{8,10},{10,8},{12,14},{14,12},{1,3},{3,1},... | collective-permute-start | bytes 405512 | tf_op jit(solution)/shard_map/ppermute | solution.py:316
  15.1 10.0 %collective-permute-start.6 = (f32[1,264,128]{2,1,0:T(8,128)S(1)}, f32[1,264,128]{2,1,0:T(8,128)S(1)}, u32[]{:S(2)}, u32[]{:S(2)}) collective-permute-start(f32[1,264,128]{2,1,0:T(8,128)S(1)} %add.14), channel_id=1, source_target_pairs={{0,4},{2,6},{4,0},{6,2},{8,12},{10,14},{12,8},{14,10},{1,5},{3,7},... | collective-permute-start | bytes 405512 | tf_op jit(solution)/shard_map/ppermute | solution.py:319
  18.0 12.4 %collective-permute-start.2 = (f32[1,264,128]{2,1,0:T(8,128)S(1)}, f32[1,264,128]{2,1,0:T(8,128)S(1)}, u32[]{:S(2)}, u32[]{:S(2)}) collective-permute-start(f32[1,264,128]{2,1,0:T(8,128)S(1)} %add.12), channel_id=1, source_target_pairs={{0,8},{2,10},{4,12},{6,14},{8,0},{10,2},{12,4},{14,6},{1,9},{3,11}... | collective-permute-start | bytes 405512 | tf_op jit(solution)/shard_map/ppermute | solution.py:319
  21.2 9.2 %collective-permute-start.4 = (f32[1,264,128]{2,1,0:T(8,128)S(1)}, f32[1,264,128]{2,1,0:T(8,128)S(1)}, u32[]{:S(2)}, u32[]{:S(2)}) collective-permute-start(f32[1,264,128]{2,1,0:T(8,128)S(1)} %add.13), channel_id=1, source_target_pairs={{0,12},{2,14},{4,8},{6,10},{8,4},{10,6},{12,0},{14,2},{1,13},{3,15... | collective-permute-start | bytes 405512 | tf_op jit(solution)/shard_map/ppermute | solution.py:319
where the time goes:
time: 32.2 us; the launch traced here: 31.8 us
  starting transfers between devices  14.7 us (46%)
  waiting for transfers between devices  8.36 us (26%)
  Pallas kernels  7.27 us (23%)
  other arithmetic  1.31 us (4%)
    ppermute x3, starting transfers between devices, steps(): total = lax.ppermute(total, 'expo', hop_pairs((d, 0)))  9.19 us
    pallas_call x4, Pallas kernels, call(): pl.pallas_call(body, out_shape=[jax.ShapeDtypeStruct(shape, jnp.float32)...  7.27 us
    ppermute x3, waiting for transfers between devices, steps(): total = lax.ppermute(total, 'expo', hop_pairs((d, 0)))  5.29 us
    ppermute x4, starting transfers between devices, steps(): moved = lax.ppermute(parts[d, i], 'expo', hop_pairs((0, i)))  5 us
    ppermute x4, waiting for transfers between devices, steps(): moved = lax.ppermute(parts[d, i], 'expo', hop_pairs((0, i)))  3.07 us
    another operation x2, other arithmetic, steps(): own = jnp.stack([science * weighted, weighted])  1.24 us
  transfers between devices with their start and end apart: 8, of which 3 were waited for; matrix products, arithmetic and copies ran while one was open for 0% of the time, Pallas kernels for 5%

commit v1 on v0

--- a/solution.py
+++ b/solution.py
@@ -135,40 +135,23 @@
         out[p, row : row + 2, :] = edges[c][0:2, :]
 
 
-def stack_targets(outs, hops, inner, wide, edge, offset_ref, shift_ref, sky, rows, chunks, lane):
+def stack_targets(outs, hops, wide, edge, offset_ref, shift_ref, sky, rows, chunks, lane):
     me = lax.axis_index("expo")
-    count = lax.axis_size("expo")
     for out, hop in zip(outs, hops):
-        owner = target_of(me, hop, count, inner)
+        owner = jnp.bitwise_xor(me, jnp.where(sky == 0, hop, turned(hop)))
         for p in range(out.shape[0]):
             stack_velocity(
                 out, p, owner * out.shape[0] + p, wide, edge, offset_ref, shift_ref, sky, rows, chunks, lane
             )
 
 
-def target_of(index, hop, count, inner):
-    far, near = hop
-    outer = count // inner
-    low = lax.rem(index, inner)
-    high = lax.div(index, inner)
-    if outer & (outer - 1) == 0:
-        high = lax.bitwise_xor(high, jnp.int32(far))
-    else:
-        high = lax.rem(high + far, outer)
-    return high * inner + lax.rem(low + near, inner)
-
-
-def owner_index(index, hop, count, inner):
-    far, near = hop
-    outer = count // inner
-    high, low = divmod(index, inner)
-    high = high ^ far if outer & (outer - 1) == 0 else (high + far) % outer
-    return high * inner + (low + near) % inner
+def turned(hop):
+    return (hop & ~3) | ((hop & 1) << 1) | ((hop >> 1) & 1)
 
 
 def far_kernel(
     spread_ref, offset_ref, shift_ref, other_ref, image_in, wide_in, image, wide, edge, *outs,
-    hops, inner, rows, chunks, taps,
+    hops, rows, chunks, taps,
 ):
     exposures = other_ref.shape[1]
     sky = lax.axis_index("sky")
@@ -192,13 +175,13 @@
             for k in range(2):
                 for c in range(chunks):
                     edge[e, t, 1 + c, k : k + 1, :] = wide[e, k, 1 + c, pl.ds(rows * t + at_row, 1), :]
-    stack_targets(outs, hops, inner, wide, edge, offset_ref, shift_ref, sky, rows, chunks, lane)
-
-
-def rest_kernel(offset_ref, shift_ref, wide, edge, *outs, hops, inner, rows, chunks):
+    stack_targets(outs, hops, wide, edge, offset_ref, shift_ref, sky, rows, chunks, lane)
+
+
+def rest_kernel(offset_ref, shift_ref, wide, edge, *outs, hops, rows, chunks):
     sky = lax.axis_index("sky")
     lane = lax.broadcasted_iota(jnp.int32, (SUB, LANES), 1)
-    stack_targets(outs, hops, inner, wide, edge, offset_ref, shift_ref, sky, rows, chunks, lane)
+    stack_targets(outs, hops, wide, edge, offset_ref, shift_ref, sky, rows, chunks, lane)
 
 
 def trail_kernel_body(trail_ref, *rest, rows, chunks, taps):
@@ -267,8 +250,6 @@
     trail_taps = trail_kernel.shape[-1]
     count = lax.axis_size("expo")
     per = tile_offset.shape[0] // count
-    inner = 2 if count % 2 == 0 else 1
-    outer = count // inner
 
     weighted = inv_variance * pixel_masks.astype(jnp.float32)
     own = jnp.stack([science * weighted, weighted])
@@ -286,14 +267,9 @@
         functools.partial(near_kernel, rows=rows, chunks=chunks, taps=taps),
         [image_shape, wide_shape], [spread, (VMEM, own)],
     )
-    far_order = far_first(outer)
-    sends = [(d, i) for d in far_order for i in range(1, inner)]
-    keeps = [(d, 0) for d in far_order]
-    early = sends[:2] if inner > 1 else keeps[:1]
-    late = [hop for hop in keeps + sends if hop not in early]
-    late = sorted(late, key=lambda hop: far_order.index(hop[0]))
+    early, late = sending_order(count)
     results = call(
-        functools.partial(far_kernel, hops=early, inner=inner, rows=rows, chunks=chunks, taps=taps),
+        functools.partial(far_kernel, hops=early, rows=rows, chunks=chunks, taps=taps),
         [image_shape, wide_shape, edge_shape] + [part] * len(early),
         [spread, offsets, shifts, (VMEM, other), (VMEM, image), (VMEM, wide)],
         aliases={4: 0, 5: 1},
@@ -301,34 +277,34 @@
     wide, edge = results[1:3]
     parts = dict(zip(early, results[3:]))
     results = call(
-        functools.partial(rest_kernel, hops=late, inner=inner, rows=rows, chunks=chunks),
+        functools.partial(rest_kernel, hops=late, rows=rows, chunks=chunks),
         [part] * len(late), [offsets, shifts, (VMEM, wide), (VMEM, edge)],
     )
     parts.update(zip(late, results))
 
-    def hop_pairs(hop):
-        return [(i, int(owner_index(i, hop, count, inner))) for i in range(count)]
-
-    arrived = []
-    for d in far_order:
-        total = parts[(d, 0)]
-        for i in range(1, inner):
-            moved = lax.ppermute(parts[(d, i)], "expo", hop_pairs((0, i)))
-            total = total + moved
-        if d:
-            total = lax.ppermute(total, "expo", hop_pairs((d, 0)))
-        arrived.append(total)
+    bit = 1
+    while bit < count:
+        pairs = [
+            (2 * i + core, 2 * (i ^ (turned(bit) if core else bit)) + core)
+            for i in range(count) for core in range(2)
+        ]
+        for hop in range(count - bit, 0, -2 * bit):
+            moved = lax.ppermute(parts[hop], ("expo", "sky"), pairs)
+            parts[hop - bit] = parts[hop - bit] + moved
+        bit *= 2
+    total = parts[0]
 
     return call(
         functools.partial(trail_kernel_body, rows=rows, chunks=chunks, taps=trail_taps),
         [(per, rows, width)],
-        [(SMEM, jnp.transpose(trail_kernel, (1, 0, 2)))] + [(VMEM, value) for value in arrived],
+        [(SMEM, jnp.transpose(trail_kernel, (1, 0, 2)))] + [(VMEM, total)],
         scratch=[pltpu.VMEM((chunks, rows + 2 * SUB, LANES), jnp.float32)],
     )[0]
 
 
-def far_first(outer):
-    return sorted(range(outer), key=lambda d: (2 * d < outer, d if 2 * d >= outer else -d))
+def sending_order(count):
+    hops = list(range(count - 1, 0, -2)) + list(range(count - 2, -1, -2))
+    return hops[:2], hops[2:]
 
 
 def solution(mesh):

time: 32.2 us -> 28.8 us (0.89)
  starting transfers between devices: 14.7 us -> 13.1 us
  waiting for transfers between devices: 8.36 us -> 6.85 us
    ppermute x7, starting transfers between devices: 14.2 us -> 12.5 us  [steps(): moved = lax.ppermute(parts[hop], ('expo', 'sky'), pairs)]
    ppermute x7, waiting for transfers between devices: 8.36 us -> 6.84 us  [steps(): moved = lax.ppermute(parts[hop], ('expo', 'sky'), pairs)]
  transfers between devices with their start and end apart: 8 -> 8, of which waited for: 3 -> 4; matrix products, arithmetic and copies ran while one was open for 0% -> 0% of each run, Pallas kernels for 5% -> 12%
where the time goes in v1:
time: 28.8 us; the launch traced here: 28.6 us
  starting transfers between devices  13.1 us (45%)
  Pallas kernels  7.24 us (25%)
  waiting for transfers between devices  6.85 us (24%)
  other arithmetic  1.33 us (5%)
    ppermute x7, starting transfers between devices, steps(): moved = lax.ppermute(parts[hop], ('expo', 'sky'), pairs)  12.5 us
    pallas_call x4, Pallas kernels, call(): pl.pallas_call(body, out_shape=[jax.ShapeDtypeStruct(shape, jnp.float32)...  7.24 us
    ppermute x7, waiting for transfers between devices, steps(): moved = lax.ppermute(parts[hop], ('expo', 'sky'), pairs)  6.84 us
    another operation x2, other arithmetic, steps(): own = jnp.stack([science * weighted, weighted])  1.24 us
  transfers between devices with their start and end apart: 8, of which 4 were waited for; matrix products, arithmetic and copies ran while one was open for 0% of the time, Pallas kernels for 12%

profile of v1, /device:TPU:0, one launch (start us, length us, event | category | flops | bytes accessed | tf_op | source)
XLA Modules:
  0.0 28.6 jit_solution(14569114056325302016)
XLA Ops:
  0.0 0.0 copy-start
  0.0 0.0 copy-start.2
  0.0 0.0 copy-start.1
  0.0 1.2 %multiply_bitcast_fusion = (f32[1,4,32,512]{3,2,1,0:T(8,128)S(1)}, f32[1,4,32,512]{3,2,1,0:T(8,128)S(1)}) fusion(f32[4,32,512]{2,1,0:T(8,128)} %param.7, f32[4,32,512]{2,1,0:T(8,128)} %param.8, s32[4,32,512]{2,1,0:T(8,128)} %param.9), kind=kLoop, calls=%fused_computation.1 | loop fusion | flops 196608 | bytes 1310720 | tf_op jit(solution)/shard_map/stack | solution.py:255
  1.3 0.6 %collective-permute-start = (f32[2,4,32,512]{3,2,1,0:T(8,128)S(1)}, f32[2,4,32,512]{3,2,1,0:T(8,128)S(1)}, u32[]{:S(2)}, u32[]{:S(2)}) collective-permute-start(f32[2,4,32,512]{3,2,1,0:T(8,128)S(1)} %pad_maximum_fusion.own_ref), channel_id=1, source_target_pairs={{0,1},{1,0},{2,3},{3,2},{4,5},{5,4},{6,7},{7,6},{8,9},{9,8},{10,11... | collective-permute-start | bytes 1572872 | tf_op jit(solution)/shard_map/ppermute | solution.py:256
  1.8 0.0 copy-done
  1.8 1.5 %shard_map.73 = (f32[2,4,4,80,128]{4,3,2,1,0:T(8,128)S(1)}, f32[4,2,7,64,128]{4,3,2,1,0:T(8,128)S(1)}) custom-call(f32[5,4,5]{2,1,0:T(4,128)S(1)} %bitcast.8, f32[2,4,32,512]{3,2,1,0:T(8,128)S(1)} %pad_maximum_fusion.own_ref), custom_call_target="tpu_custom_call" | custom-call | tf_op jit(solution)/shard_map/pallas_call | solution.py:233
  3.4 0.0 collective-permute-done.other_ref
  3.4 0.0 copy-done.2
  3.4 0.0 copy-done.1
  3.4 2.5 %shard_map.74 = (f32[2,4,4,80,128]{4,3,2,1,0:T(8,128)S(1)}, f32[4,2,7,64,128]{4,3,2,1,0:T(8,128)S(1)}, f32[4,2,7,8,128]{4,3,2,1,0:T(8,128)S(1)}, f32[1,264,128]{2,1,0:T(8,128)S(1)}, f32[1,264,128]{2,1,0:T(8,128)S(1)}) custom-call(f32[5,4,5]{2,1,0:T(4,128)S(1)} %bitcast.9, s32[4,8]{1,0:T(4,128)S(1)} %bitcast.10, ...), custom_call_target="tpu_custom_call", output_to_operand_aliasing={{0}: (4, {}), {1}: (5, {})} | custom-call | tf_op jit(solution)/shard_map/pallas_call | solution.py:233
  5.9 2.9 %collective-permute-start.5 = (f32[1,264,128]{2,1,0:T(8,128)S(1)}, f32[1,264,128]{2,1,0:T(8,128)S(1)}, u32[]{:S(2)}, u32[]{:S(2)}) collective-permute-start(f32[1,264,128]{2,1,0:T(8,128)S(1)} %get-tuple-element.28), channel_id=1, source_target_pairs={{0,2},{1,5},{2,0},{3,7},{4,6},{5,1},{6,4},{7,3},{8,10},{9,13},{10,... | collective-permute-start | bytes 405512 | tf_op jit(solution)/shard_map/ppermute | solution.py:292
  8.8 0.0 copy-start.3
  8.8 1.8 %shard_map.75 = (f32[1,264,128]{2,1,0:T(8,128)S(1)}, f32[1,264,128]{2,1,0:T(8,128)S(1)}, f32[1,264,128]{2,1,0:T(8,128)S(1)}, f32[1,264,128]{2,1,0:T(8,128)S(1)},...) custom-call(s32[4,8]{1,0:T(4,128)S(1)} %bitcast.11, s32[4,8]{1,0:T(4,128)S(1)} %bitcast.13, ...), custom_call_target="tpu_custom_call" | custom-call | tf_op jit(solution)/shard_map/pallas_call | solution.py:233
  10.6 0.1 collective-permute-start.2
  10.7 2.0 %collective-permute-start.4 = (f32[1,264,128]{2,1,0:T(8,128)S(1)}, f32[1,264,128]{2,1,0:T(8,128)S(1)}, u32[]{:S(2)}, u32[]{:S(2)}) collective-permute-start(f32[1,264,128]{2,1,0:T(8,128)S(1)} %get-tuple-element.26), channel_id=1, source_target_pairs={{0,2},{1,5},{2,0},{3,7},{4,6},{5,1},{6,4},{7,3},{8,10},{9,13},{10,... | collective-permute-start | bytes 405512 | tf_op jit(solution)/shard_map/ppermute | solution.py:292
  12.7 0.0 collective-permute-done.5
  12.8 1.6 %collective-permute-start.6 = (f32[1,264,128]{2,1,0:T(8,128)S(1)}, f32[1,264,128]{2,1,0:T(8,128)S(1)}, u32[]{:S(2)}, u32[]{:S(2)}) collective-permute-start(f32[1,264,128]{2,1,0:T(8,128)S(1)} %add.25), channel_id=1, source_target_pairs={{0,4},{1,3},{2,6},{3,1},{4,0},{5,7},{6,2},{7,5},{8,12},{9,11},{10,... | collective-permute-start | bytes 405512 | tf_op jit(solution)/shard_map/ppermute | solution.py:292
  14.4 1.1 %collective-permute-start.1 = (f32[1,264,128]{2,1,0:T(8,128)S(1)}, f32[1,264,128]{2,1,0:T(8,128)S(1)}, u32[]{:S(2)}, u32[]{:S(2)}) collective-permute-start(f32[1,264,128]{2,1,0:T(8,128)S(1)} %get-tuple-element.22), channel_id=1, source_target_pairs={{0,2},{1,5},{2,0},{3,7},{4,6},{5,1},{6,4},{7,3},{8,10},{9,13},{10,... | collective-permute-start | bytes 405512 | tf_op jit(solution)/shard_map/ppermute | solution.py:292
  15.5 1.2 %collective-permute-done.2 = f32[1,264,128]{2,1,0:T(8,128)S(1)} collective-permute-done((f32[1,264,128]{2,1,0:T(8,128)S(1)}, f32[1,264,128]{2,1,0:T(8,128)S(1)}, u32[]{:S(2)}, u32[]{:S(2)}) %collective-permute-start.2) | collective-permute-done | bytes 135200 | tf_op jit(solution)/shard_map/ppermute | solution.py:292
  16.7 2.2 %collective-permute-start.3 = (f32[1,264,128]{2,1,0:T(8,128)S(1)}, f32[1,264,128]{2,1,0:T(8,128)S(1)}, u32[]{:S(2)}, u32[]{:S(2)}) collective-permute-start(f32[1,264,128]{2,1,0:T(8,128)S(1)} %add.22), channel_id=1, source_target_pairs={{0,4},{1,3},{2,6},{3,1},{4,0},{5,7},{6,2},{7,5},{8,12},{9,11},{10,... | collective-permute-start | bytes 405512 | tf_op jit(solution)/shard_map/ppermute | solution.py:292
  18.8 0.7 %collective-permute-done.4 = f32[1,264,128]{2,1,0:T(8,128)S(1)} collective-permute-done((f32[1,264,128]{2,1,0:T(8,128)S(1)}, f32[1,264,128]{2,1,0:T(8,128)S(1)}, u32[]{:S(2)}, u32[]{:S(2)}) %collective-permute-start.4) | collective-permute-done | bytes 135200 | tf_op jit(solution)/shard_map/ppermute | solution.py:292
  19.5 0.0 collective-permute-done.6
  19.6 2.7 %collective-permute-start.7 = (f32[1,264,128]{2,1,0:T(8,128)S(1)}, f32[1,264,128]{2,1,0:T(8,128)S(1)}, u32[]{:S(2)}, u32[]{:S(2)}) collective-permute-start(f32[1,264,128]{2,1,0:T(8,128)S(1)} %add_add_fusion), channel_id=1, source_target_pairs={{0,8},{1,9},{2,10},{3,11},{4,12},{5,13},{6,14},{7,15},{8,0},{9,1},... | collective-permute-start | bytes 405512 | tf_op jit(solution)/shard_map/ppermute | solution.py:292
  22.2 0.0 collective-permute-done.1
  22.2 0.2 collective-permute-done.3
  22.4 4.8 %collective-permute-done.7 = f32[1,264,128]{2,1,0:T(8,128)S(1)} collective-permute-done((f32[1,264,128]{2,1,0:T(8,128)S(1)}, f32[1,264,128]{2,1,0:T(8,128)S(1)}, u32[]{:S(2)}, u32[]{:S(2)}) %collective-permute-start.7) | collective-permute-done | bytes 135200 | tf_op jit(solution)/shard_map/ppermute | solution.py:292
  27.2 0.0 copy-done.3
  27.2 1.4 %shard_map.76 = f32[1,32,512]{2,1,0:T(8,128)} custom-call(f32[3,1,3]{2,1,0:T(1,128)S(1)} %bitcast.14, f32[1,264,128]{2,1,0:T(8,128)S(1)} %add_add_fusion.1.rest_0_), custom_call_target="tpu_custom_call" | custom-call | tf_op jit(solution)/shard_map/pallas_call | solution.py:233
  (5 shorter events, 0.1 us)
Async XLA Ops:
  0.0 1.8 %copy-start = (f32[4,5,5]{2,0,1:T(4,128)S(1)}, f32[4,5,5]{2,0,1:T(4,128)}, u32[]{:S(2)}) copy-start(f32[4,5,5]{2,0,1:T(4,128)} %param.10) | copy-start | bytes 1204
  0.0 3.4 %copy-start.2 = (s32[8,4]{0,1:T(4,128)S(1)}, s32[8,4]{0,1:T(4,128)}, u32[]{:S(2)}) copy-start(s32[8,4]{0,1:T(4,128)} %param.12) | copy-start | bytes 388
  0.0 3.4 %copy-start.1 = (s32[8,4]{0,1:T(4,128)S(1)}, s32[8,4]{0,1:T(4,128)}, u32[]{:S(2)}) copy-start(s32[8,4]{0,1:T(4,128)} %param.11) | copy-start | bytes 388
  1.3 2.1 %collective-permute-start = (f32[2,4,32,512]{3,2,1,0:T(8,128)S(1)}, f32[2,4,32,512]{3,2,1,0:T(8,128)S(1)}, u32[]{:S(2)}, u32[]{:S(2)}) collective-permute-start(f32[2,4,32,512]{3,2,1,0:T(8,128)S(1)} %pad_maximum_fusion.own_ref), channel_id=1, source_target_pairs={{0,1},{1,0},{2,3},{3,2},{4,5},{5,4},{6,7},{7,6},{8,9},{9,8},{10,11... | collective-permute-start | bytes 1572872 | tf_op jit(solution)/shard_map/ppermute | solution.py:256
  5.9 6.8 %collective-permute-start.5 = (f32[1,264,128]{2,1,0:T(8,128)S(1)}, f32[1,264,128]{2,1,0:T(8,128)S(1)}, u32[]{:S(2)}, u32[]{:S(2)}) collective-permute-start(f32[1,264,128]{2,1,0:T(8,128)S(1)} %get-tuple-element.28), channel_id=1, source_target_pairs={{0,2},{1,5},{2,0},{3,7},{4,6},{5,1},{6,4},{7,3},{8,10},{9,13},{10,... | collective-permute-start | bytes 405512 | tf_op jit(solution)/shard_map/ppermute | solution.py:292
  8.8 18.4 %copy-start.3 = (f32[1,3,3]{2,0,1:T(1,128)S(1)}, f32[1,3,3]{2,0,1:T(1,128)}, u32[]{:S(2)}) copy-start(f32[1,3,3]{2,0,1:T(1,128)} %param.13) | copy-start | bytes 112
  10.6 6.0 %collective-permute-start.2 = (f32[1,264,128]{2,1,0:T(8,128)S(1)}, f32[1,264,128]{2,1,0:T(8,128)S(1)}, u32[]{:S(2)}, u32[]{:S(2)}) collective-permute-start(f32[1,264,128]{2,1,0:T(8,128)S(1)} %get-tuple-element.24), channel_id=1, source_target_pairs={{0,2},{1,5},{2,0},{3,7},{4,6},{5,1},{6,4},{7,3},{8,10},{9,13},{10,... | collective-permute-start | bytes 405512 | tf_op jit(solution)/shard_map/ppermute | solution.py:292
  10.7 8.8 %collective-permute-start.4 = (f32[1,264,128]{2,1,0:T(8,128)S(1)}, f32[1,264,128]{2,1,0:T(8,128)S(1)}, u32[]{:S(2)}, u32[]{:S(2)}) collective-permute-start(f32[1,264,128]{2,1,0:T(8,128)S(1)} %get-tuple-element.26), channel_id=1, source_target_pairs={{0,2},{1,5},{2,0},{3,7},{4,6},{5,1},{6,4},{7,3},{8,10},{9,13},{10,... | collective-permute-start | bytes 405512 | tf_op jit(solution)/shard_map/ppermute | solution.py:292
  12.8 6.8 %collective-permute-start.6 = (f32[1,264,128]{2,1,0:T(8,128)S(1)}, f32[1,264,128]{2,1,0:T(8,128)S(1)}, u32[]{:S(2)}, u32[]{:S(2)}) collective-permute-start(f32[1,264,128]{2,1,0:T(8,128)S(1)} %add.25), channel_id=1, source_target_pairs={{0,4},{1,3},{2,6},{3,1},{4,0},{5,7},{6,2},{7,5},{8,12},{9,11},{10,... | collective-permute-start | bytes 405512 | tf_op jit(solution)/shard_map/ppermute | solution.py:292
  14.4 7.8 %collective-permute-start.1 = (f32[1,264,128]{2,1,0:T(8,128)S(1)}, f32[1,264,128]{2,1,0:T(8,128)S(1)}, u32[]{:S(2)}, u32[]{:S(2)}) collective-permute-start(f32[1,264,128]{2,1,0:T(8,128)S(1)} %get-tuple-element.22), channel_id=1, source_target_pairs={{0,2},{1,5},{2,0},{3,7},{4,6},{5,1},{6,4},{7,3},{8,10},{9,13},{10,... | collective-permute-start | bytes 405512 | tf_op jit(solution)/shard_map/ppermute | solution.py:292
  16.7 5.7 %collective-permute-start.3 = (f32[1,264,128]{2,1,0:T(8,128)S(1)}, f32[1,264,128]{2,1,0:T(8,128)S(1)}, u32[]{:S(2)}, u32[]{:S(2)}) collective-permute-start(f32[1,264,128]{2,1,0:T(8,128)S(1)} %add.22), channel_id=1, source_target_pairs={{0,4},{1,3},{2,6},{3,1},{4,0},{5,7},{6,2},{7,5},{8,12},{9,11},{10,... | collective-permute-start | bytes 405512 | tf_op jit(solution)/shard_map/ppermute | solution.py:292
  19.6 7.6 %collective-permute-start.7 = (f32[1,264,128]{2,1,0:T(8,128)S(1)}, f32[1,264,128]{2,1,0:T(8,128)S(1)}, u32[]{:S(2)}, u32[]{:S(2)}) collective-permute-start(f32[1,264,128]{2,1,0:T(8,128)S(1)} %add_add_fusion), channel_id=1, source_target_pairs={{0,8},{1,9},{2,10},{3,11},{4,12},{5,13},{6,14},{7,15},{8,0},{9,1},... | collective-permute-start | bytes 405512 | tf_op jit(solution)/shard_map/ppermute | solution.py:292
